TPU v7x, 256 devices: a 2x2x32 block of a 4x8x32 slice. The times are simulated.
256 devices in a mesh: parts: 4 (over x, y), pts: 64 (over z, core).
Axes of the slice: x: 2, y: 2, z: 32, core: 2. Of those that a mesh axis runs over, the one named last changes fastest.
The devices are a block of a 4x8x32 slice.
Arguments:
- grid_weights: float32 [512, 128, 128], P(('parts', 'pts')), parts along dimension 0, may hold values from -6 to 6
- direction: float32 [512, 128, 128], P(('parts', 'pts')), parts along dimension 0, may hold values from -6 to 6
- kern_x: float32 [128, 128], replicated
- kern_y: float32 [128, 128], replicated
- kern_z: float32 [128, 128], replicated
- interp: bfloat16 [32768, 128, 256], P(('parts', 'pts')), parts along dimension 0, may hold values from -4 to 4
- block_corner: int32 [3, 32768], P(None, ('parts', 'pts')), parts along dimension 1, may hold values from 0 to 120, as said below
- block_offsets: int32 [32768, 256], P(('parts', 'pts')), parts along dimension 0, may hold values from 0 to 2047, as said below
- labels: int32 [32768, 128], P(('parts', 'pts')), parts along dimension 0, may hold values 0 or 1
- trial_steps: float32 [5], replicated, may hold values from 0.05 to 2
- accept: int32 [1], replicated, may hold values from 0 to 4
Outputs:
- new_weights: float32 [512, 128, 128], P(('parts', 'pts')), parts along dimension 0
- grid_gradient: float32 [512, 128, 128], P(('parts', 'pts')), parts along dimension 0
- curvature: float32 [32768, 128], P(('parts', 'pts')), parts along dimension 0
- trial_objective: float32 [20], P('parts'), parts along dimension 0
- trial_slope: float32 [20], P('parts'), parts along dimension 0
There are 4 independent parts, one for each index of `parts`. A program takes and returns all parts, laid end to end along the dimension named above; an argument that names none is the same for every part. Nothing has to cross between parts.
Inputs may be any that keep to these rules, and one draw needn't show every extreme that they name: `block_corner`: row 0 lies in 0 to 112, row 1 in 0 to 112, row 2 in 0 to 120. `block_offsets`: the 256 offsets of one block are distinct.
All inputs are finite; a program needn't handle non-finite values. No bound on the sum of `labels` on one device may be relied on, other than what follows from the above.
Results may differ from a plain program's by a relative error of at most 0.0075.
The roundings to bfloat16 on the way count: a program that leaves them out, or rounds other values in their place, can miss the bound.
Values may be sent and summed in bfloat16 or wider, within the bound.
A program may use at most 128 MiB of HBM per device.

v0:
```python
import jax
import jax.numpy as jnp
from jax import lax
from jax.sharding import Mesh
from jax.sharding import PartitionSpec as P

BOXY = 16
BOXZ = 8
NTRIAL = 5
PTS = ("pts_0", "pts_1")
PARTS_PTS = ("parts", "pts_0", "pts_1")


HIGHEST = lax.Precision.HIGHEST


def by_axis(array, axes):
    for axis in axes:
        array = lax.psum(array, axis)
    return array


def sum_in_order(tiles, axes, order):
    inside = tiles.shape[1:]
    tiles = tiles.reshape(*(lax.axis_size(a) for a in axes), *inside)
    tiles = jnp.moveaxis(tiles, order, range(len(axes))).reshape(-1, *inside)
    for k in order:
        tiles = lax.psum_scatter(tiles, axes[k], scatter_dimension=0, tiled=True)
    return tiles[0]


def in_blocks(array, dim, count):
    lengths = array.shape
    tiles = array.reshape(*lengths[:dim], count, lengths[dim] // count, *lengths[dim + 1 :])
    return jnp.moveaxis(tiles, dim, 0)


def scatter_axes(array, axes, order, dim):
    count = lax.axis_size(axes)
    return sum_in_order(in_blocks(array, dim, count), axes, order)


def plane_mix(fields, kern_y, kern_z):
    inner_mix = jnp.einsum("...bc,zc->...bz", fields, kern_z, precision=HIGHEST)
    return jnp.einsum("...xbz,yb->...xyz", inner_mix, kern_y, precision=HIGHEST).astype(
        jnp.bfloat16
    )


def depth_mix(partial_value, kern_x):
    return jnp.einsum(
        "xa,...ayz->...xyz", kern_x, partial_value.astype(jnp.float32), precision=HIGHEST
    )


def cell_parts_of(block_corner, block_offsets, size_y):
    plane_off = block_offsets // (BOXY * BOXZ)
    row_off = block_offsets // BOXZ % BOXY
    depth_off = block_offsets % BOXZ
    cell_x = block_corner[0][:, None] + plane_off
    cell_y = block_corner[1][:, None] + row_off
    cell_z = block_corner[2][:, None] + depth_off
    return (cell_x * size_y + cell_y, cell_z)


def pick_cells(grid_rows, row_ids, depth_ids):
    depth_size = grid_rows.shape[-1]
    taken = jnp.take(grid_rows, row_ids, axis=1)
    depth_line = lax.broadcasted_iota(jnp.int32, (1, 1, depth_size), 2)
    wanted = depth_ids[:, :, None] == depth_line
    kept = jnp.where(wanted[None], taken, jnp.zeros((), taken.dtype))
    return jnp.sum(kept.astype(jnp.float32), axis=-1).astype(jnp.bfloat16)


def slab_add(row_ids, depth_ids, flat_terms, row_count, size_y, size_z):
    inside = (row_ids >= 0) & (row_ids < row_count * size_y)
    target_row = jnp.where(inside, row_ids, row_count * size_y)
    depth_line = lax.broadcasted_iota(jnp.int32, (1, size_z), 1)
    placed = jnp.where(depth_ids[:, None] == depth_line, flat_terms[:, None], 0.0)
    summed = (
        jnp.zeros((row_count * size_y, size_z), jnp.float32).at[target_row].add(placed, mode="drop")
    )
    return summed.reshape(row_count, size_y, size_z)


def kron_apply(fields, kern_x, kern_y, kern_z):
    partial_value = plane_mix(fields, kern_y, kern_z)
    slab_rows = fields.shape[1]
    gathered = lax.all_gather(partial_value, PTS, axis=1, tiled=True)
    mixed_grid = depth_mix(gathered, kern_x)
    slab_part = lax.dynamic_slice_in_dim(mixed_grid, lax.axis_index(PTS) * slab_rows, slab_rows, 1)
    return (slab_part, mixed_grid.astype(jnp.bfloat16))


def body(
    grid_weights,
    direction,
    kern_x,
    kern_y,
    kern_z,
    interp,
    block_corner,
    block_offsets,
    labels,
    trial_steps,
    accept,
):
    slab_rows, size_y, size_z = grid_weights.shape
    devices = lax.axis_size(PTS)
    points = interp.shape[0] * interp.shape[1] * devices
    row_ids, depth_ids = cell_parts_of(block_corner, block_offsets, size_y)
    slab_pair, whole_pair = kron_apply(jnp.stack([grid_weights, direction]), kern_x, kern_y, kern_z)
    quad_local = jnp.stack(
        [
            jnp.sum(grid_weights * slab_pair[0]),
            jnp.sum(direction * slab_pair[0]),
            jnp.sum(direction * slab_pair[1]),
        ]
    )
    values = pick_cells(whole_pair.reshape(2, -1, size_z), row_ids, depth_ids)
    latent_pair = jnp.einsum("bpc,fbc->fbp", interp, values, preferred_element_type=jnp.float32)
    latent = latent_pair[0]
    slope_pt = latent_pair[1]
    target = labels.astype(jnp.float32)
    signed = 2.0 * target - 1.0
    trial_latent = latent[None] + trial_steps[:, None, None] * slope_pt[None]
    loglik_local = jnp.sum(jax.nn.log_sigmoid(signed[None] * trial_latent), axis=(1, 2))
    descent_local = jnp.sum(
        (target[None] - jax.nn.sigmoid(trial_latent)) * slope_pt[None], axis=(1, 2)
    )
    quadratics, loglik, descent = (
        by_axis(quad_local, PTS),
        by_axis(loglik_local, PTS),
        by_axis(descent_local, PTS),
    )
    prior = 0.5 * (
        quadratics[0]
        + 2.0 * trial_steps * quadratics[1]
        + trial_steps * trial_steps * quadratics[2]
    )
    trial_objective = (loglik - prior) / points
    trial_slope = (descent - quadratics[1] - trial_steps * quadratics[2]) / points
    chosen = jnp.sum(jnp.where(jnp.arange(NTRIAL) == accept[0], trial_steps, 0.0))
    probability = jax.nn.sigmoid(latent + chosen * slope_pt)
    residual = (target - probability).astype(jnp.bfloat16)
    column_term = jnp.einsum("bpc,bp->bc", interp, residual, preferred_element_type=jnp.float32)
    flat_rows = row_ids.reshape(-1)
    flat_depths = depth_ids.reshape(-1)
    flat_terms = column_term.reshape(-1)
    spread = scatter_axes(
        slab_add(
            flat_rows, flat_depths, flat_terms, slab_rows * lax.axis_size(PTS), size_y, size_z
        ),
        PTS,
        (1, 0),
        0,
    )
    new_weights = grid_weights + chosen * direction
    grid_gradient = spread - new_weights
    unused_slab, bend_whole = kron_apply(grid_gradient[None], kern_x, kern_y, kern_z)
    bend_values = pick_cells(bend_whole.reshape(1, -1, size_z), row_ids, depth_ids)
    bend_pt = jnp.einsum("bpc,fbc->fbp", interp, bend_values, preferred_element_type=jnp.float32)[0]
    curvature = probability * (1.0 - probability) * bend_pt
    return (new_weights, grid_gradient, curvature, trial_objective, trial_slope)


def solution(mesh):
    finer = Mesh(mesh.devices.reshape(mesh.shape["parts"], 32, 2), ("parts", "pts_0", "pts_1"))
    placed = (
        P(PARTS_PTS, None, None),
        P(PARTS_PTS, None, None),
        P(),
        P(),
        P(),
        P(PARTS_PTS, None, None),
        P(None, PARTS_PTS),
        P(PARTS_PTS, None),
        P(PARTS_PTS, None),
        P(),
        P(),
    )
    return jax.shard_map(
        body,
        mesh=finer,
        in_specs=placed,
        out_specs=(
            P(PARTS_PTS, None, None),
            P(PARTS_PTS, None, None),
            P(PARTS_PTS, None),
            P("parts"),
            P("parts"),
        ),
        check_vma=False,
    )
```

profile of v0, /device:TPU:37, one launch (start us, length us, event | category | flops | bytes accessed | tf_op | source)
XLA Modules:
  0.0 1211.2 jit_solution(13192357690105287026)
XLA Ops:
  7.3 1.4 fusion.22
  8.6 1.9 fusion.19
  14.6 1.3 fusion.53
  16.9 6.4 iota_compare_fusion.1
  23.6 138.8 %all-gather.3.cloned.1.call-done = bf16[2,128,128,128]{2,3,1,0:T(8,128)(2,1)} async-done(((bf16[2,2,128,128]{2,3,1,0:T(8,128)(2,1)}), bf16[2,128,128,128]{2,3,1,0:T(8,128)(2,1)}) %all-gather.3.cloned.1.call-update) | async-done | bytes 8388624 | tf_op jit(solution)/shard_map/all_gather | solution.py:89
  162.4 12.4 %copy.56 = bf16[2,128,128,128]{3,1,2,0:T(8,128)(2,1)} copy(bf16[2,128,128,128]{2,3,1,0:T(8,128)(2,1)} %all-gather.3.cloned.1.call-done) | data formatting | bytes 16777216 | tf_op jit(solution)/shard_map/all_gather | solution.py:89
  174.8 9.8 fusion.42
  184.6 5.7 copy-done.1
  190.3 4.1 convert_bitcast_fusion
  194.4 12.0 copy.57
  206.4 16.4 %copy.58 = bf16[2,16384,128]{2,0,1:T(2,128)(2,1)} copy(bf16[2,16384,128]{2,1,0:T(8,128)(2,1)} %bitcast.127) | data formatting | bytes 16777216 | tf_op jit(solution)/shard_map/reshape | solution.py:120
  222.8 214.7 %gather_fusion = bf16[32768,2,128]{2,1,0:T(2,128)(2,1)} fusion(bf16[2,16384,128]{2,0,1:T(2,128)(2,1)} %copy.58, s32[32768]{0:T(1024)S(1)} %broadcast_clamp_fusion), kind=kCustom, calls=%fused_computation | custom fusion | bytes 33685504 | tf_op jit(solution)/shard_map/jit(_take)/gather | solution.py:68
  437.5 97.9 %fusion.2 = bf16[128,256,2]{2,1,0:T(8,128)(2,1)} fusion(bf16[128,256,2,128]{3,2,1,0:T(2,128)(2,1)} %bitcast.123, pred[128,256]{1,0:T(8,128)(4,1)S(1)} %get-tuple-element.18, pred[128,256,128]{2,1,0:T(8,128)(4,1)} %iota_compare_fusion.1), kind=kLoop, calls=%fused_computation.10 | loop fusion | flops 25100288 | bytes 21135360 | tf_op jit(solution)/shard_map/reduce_sum | solution.py:72
  535.3 8.1 fusion.16
  544.2 4.6 fusion.50
  548.9 198.6 %scatter_custom_fusion = f32[16384,128]{1,0:T(8,128)} fusion(s32[32768]{0:T(1024)S(1)} %bitcast.144, f32[]{:T(128)} %constant.93.clone.1, f32[32768]{0:T(1024)S(1)} %bitcast.139, s32[32768]{0:T(1024)S(1)} %bitcast.138), kind=kCustom, calls=%fused_computation.6 | custom fusion | flops 12582912 | bytes 8651776 | tf_op jit(solution)/shard_map/scatter-add | solution.py:81
  747.5 7.7 copy.61
  755.4 25.3 %reduce-scatter.3.cloned.1.call-done = f32[32,2,128,128]{3,2,1,0:T(8,128)} async-done(((f32[64,2,128,128]{3,2,1,0:T(8,128)}), f32[32,2,128,128]{3,2,1,0:T(8,128)}) %reduce-scatter.3.cloned.1.call-update) | async-done | bytes 4194320 | tf_op jit(solution)/shard_map/reduce_scatter | solution.py:28
  781.0 121.2 %reduce-scatter.5.cloned.1.call-done = f32[1,2,128,128]{3,2,1,0:T(8,128)} async-done(((f32[32,2,128,128]{3,2,1,0:T(8,128)}), f32[1,2,128,128]{3,2,1,0:T(8,128)}) %reduce-scatter.5.cloned.1.call-update) | async-done | bytes 131088 | tf_op jit(solution)/shard_map/reduce_scatter | solution.py:28
  902.3 2.2 bitcast_subtract_fusion
  906.4 1.3 dynamic-slice_bitcast_fusion
  908.7 2.1 pad_maximum_fusion
  910.7 41.6 %all-reduce = (f32[5]{0:T(128)S(1)}, f32[3]{0:T(128)S(1)}, f32[5]{0:T(128)S(1)}) all-reduce(f32[5]{0:T(128)S(1)} %neg.22, f32[3]{0:T(128)S(1)} %pad_maximum_fusion, f32[5]{0:T(128)S(1)} %get-tuple-element.8), channel_id=1, replica_groups=mesh['parts'=4,'pts_0'=32,'pts_1'=2] {'pts_0'}, use_global_device_ids=true, to_apply=%region_7.8 | all-reduce | flops 13 | bytes 104 | tf_op jit(solution)/shard_map/psum | solution.py:19
  952.3 36.3 %all-reduce.1 = (f32[5]{0:T(128)S(1)}, f32[3]{0:T(128)S(1)}, f32[5]{0:T(128)S(1)}) all-reduce(f32[5]{0:T(128)S(1)} %get-tuple-element.10, f32[3]{0:T(128)S(1)} %get-tuple-element.11, f32[5]{0:T(128)S(1)} %get-tuple-element.12), channel_id=1, replica_groups=mesh['parts'=4,'pts_0'=32,'pts_1'=2] {'pts_1'}, use_global_device_ids=true, to_apply=%region_8.9 | all-reduce | flops 13 | bytes 104 | tf_op jit(solution)/shard_map/psum | solution.py:19
  989.9 2.4 subtract_multiply_fusion.1
  992.3 65.4 %all-gather.5.cloned.1.call-done = bf16[1,128,128,128]{3,2,0,1:T(8,128)(2,1)} async-done(((bf16[1,2,128,128]{3,2,0,1:T(8,128)(2,1)}), bf16[1,128,128,128]{3,2,0,1:T(8,128)(2,1)}) %all-gather.5.cloned.1.call-update) | async-done | bytes 4194320 | tf_op jit(solution)/shard_map/all_gather | solution.py:89
  1057.8 7.2 convert_bitcast_fusion.1
  1065.0 4.7 copy.65
  1069.7 112.1 %gather_fusion.1 = bf16[32768,128]{1,0:T(8,128)(2,1)} fusion(bf16[16384,128]{1,0:T(8,128)(2,1)} %bitcast.122, s32[32768]{0:T(1024)S(1)} %broadcast_clamp_fusion), kind=kCustom, calls=%fused_computation.1 | custom fusion | bytes 16908288 | tf_op jit(solution)/shard_map/jit(_take)/gather | solution.py:68
  1181.8 15.7 %fusion.4 = bf16[128,256]{1,0:T(8,128)(2,1)S(1)} fusion(bf16[1,128,256,128]{3,2,1,0:T(8,128)(2,1)} %bitcast.124, s32[128,256]{1,0:T(8,128)S(1)} %fusion.32, pred[128,256]{1,0:T(8,128)(4,1)S(1)} %get-tuple-element.18), kind=kLoop, calls=%fused_computation.12 | loop fusion | flops 16744448 | bytes 8617984 | tf_op jit(solution)/shard_map/reduce_sum | solution.py:72
  1197.6 5.6 fusion.35
  1203.2 1.3 fusion.41
  (47 shorter events, 9.4 us)
Async XLA Ops:
  7.2 167.6 %copy-start = (f32[128,128]{1,0:T(8,128)S(1)}, f32[128,128]{1,0:T(8,128)}, u32[]{:S(2)}) copy-start(f32[128,128]{1,0:T(8,128)} %param.13) | copy-start | bytes 196612
  7.2 155.2 %all-gather.3.cloned.1.call-start = ((), (), s32[]{:S(2)}) async-start(), calls=%async_computation.2 | async-start | bytes 8519680 | tf_op jit(solution)/shard_map/all_gather | solution.py:89
  10.6 770.2 %reduce-scatter.3.cloned.1.call-start = ((), (), s32[]{:S(2)}) async-start(), calls=%async_computation.3 | async-start | bytes 12582912 | tf_op jit(solution)/shard_map/reduce_scatter | solution.py:28
  184.6 5.7 copy-start.1
  535.3 8.2 copy-start.7
  755.3 147.0 %copy-start.2 = (f32[2,128,128]{2,1,0:T(8,128)S(1)}, f32[2,128,128]{2,1,0:T(8,128)}, u32[]{:S(2)}) copy-start(f32[2,128,128]{2,1,0:T(8,128)} %param.12) | copy-start | bytes 393220
  755.3 147.0 %copy-start.3 = (f32[2,128,128]{2,1,0:T(8,128)S(1)}, f32[2,128,128]{2,1,0:T(8,128)}, u32[]{:S(2)}) copy-start(f32[2,128,128]{2,1,0:T(8,128)} %param.11) | copy-start | bytes 393220
  755.3 149.2 %copy-start.5 = (f32[128,128]{1,0:T(8,128)S(1)}, f32[128,128]{1,0:T(8,128)}, u32[]{:S(2)}) copy-start(f32[128,128]{1,0:T(8,128)} %param.15) | copy-start | bytes 196612
  755.3 149.5 %copy-start.6 = (f32[128,128]{1,0:T(8,128)S(1)}, f32[128,128]{1,0:T(8,128)}, u32[]{:S(2)}) copy-start(f32[128,128]{1,0:T(8,128)} %param.14) | copy-start | bytes 196612
  755.3 150.6 %copy-start.8 = (f32[5]{0:T(128)S(1)}, f32[5]{0:T(128)}, u32[]{:S(2)}) copy-start(f32[5]{0:T(128)} %param.20) | copy-start | bytes 64
  755.3 146.9 %reduce-scatter.5.cloned.1.call-start = ((), (), s32[]{:S(2)}) async-start(), calls=%async_computation.4 | async-start | bytes 4325376 | tf_op jit(solution)/shard_map/reduce_scatter | solution.py:28
  780.8 277.0 %all-gather.5.cloned.1.call-start = ((), (), s32[]{:S(2)}) async-start(), calls=%async_computation.5 | async-start | bytes 4259840 | tf_op jit(solution)/shard_map/all_gather | solution.py:89
  904.5 165.2 %copy-start.4 = (f32[2,128,128]{2,1,0:T(8,128)}, f32[2,128,128]{2,1,0:T(8,128)S(1)}, u32[]{:S(2)}) copy-start(f32[2,128,128]{2,1,0:T(8,128)S(1)} %get-tuple-element.16) | copy-start | bytes 393220
Sparse Core Ops, SparseCore 0:
  10.7 151.6 all-gather.2
  755.5 25.2 reduce-scatter.2
  783.3 118.9 reduce-scatter.4
  906.0 151.7 all-gather.4
where the time goes:
time: 1220 us; the launch traced here: 1210 us
  local copies, waits for them, and re-layouts  390 us (32%)
  waiting for transfers between devices  351 us (29%)
  other arithmetic  338 us (28%)
  blocking collectives  77.9 us (6%)
  matrix products  39.1 us (3%)
  between operations  15.5 us (1%)
    gather x2, local copies, waits for them, and re-layouts, pick_cells(): taken = jnp.take(grid_rows, row_ids, axis=1)  327 us
    all_gather x2, waiting for transfers between devices, kron_apply(): gathered = lax.all_gather(partial_value, PTS, axis=1, tiled=True)  204 us
    scatter-add x1, other arithmetic, slab_add(): jnp.zeros((row_count * size_y, size_z), jnp.float32).at[target_row]  199 us
    reduce_scatter x2, waiting for transfers between devices, sum_in_order(): tiles = lax.psum_scatter(tiles, axes[k], scatter_dimension=0, tiled=True)  147 us
    reduce_sum x2, other arithmetic, pick_cells(): return jnp.sum(kept.astype(jnp.float32), axis=-1).astype(jnp.bfloat16)  114 us
    psum x2, blocking collectives, by_axis(): array = lax.psum(array, axis)  77.9 us
  transfers between devices with their start and end apart: 4, of which 4 were waited for; matrix products, arithmetic and copies ran while one was open for 2% of the time, Pallas kernels for 0%

commit v1 on v0

v1 whole, which is shorter than its diff:
```python
import functools

import jax
import jax.numpy as jnp
from jax import lax
from jax.experimental import pallas as pl
from jax.experimental.pallas import tpu as pltpu
from jax.sharding import Mesh
from jax.sharding import PartitionSpec as P

BOXX = 16
BOXY = 16
BOXZ = 8
NTRIAL = 5
PTS = ("pts_0", "pts_1")
PARTS_PTS = ("parts", "pts_0", "pts_1")
HIGHEST = lax.Precision.HIGHEST
F32 = jnp.float32
BF16 = jnp.bfloat16
LINE = 136
ZC = 16
XW = 32
VMEM_CAP = 60 * 1024 * 1024
NT = (((1,), (1,)), ((), ()))


def depth_mix(fields, gath_ref, kxs_ref, lines, img_ref, on_rows):
    depth = img_ref.shape[1]
    count_a = gath_ref.shape[0]

    def chunk(k, carry):
        z0 = pl.multiple_of(k * ZC, ZC)

        def place(i, c):
            for u in range(8):
                a = i * 8 + u
                for f in range(fields):
                    lines[f][pl.ds(a, ZC, stride=LINE), :] = gath_ref[a, f, pl.ds(z0, ZC), :].astype(F32)
            return c

        lax.fori_loop(0, count_a // 8, place, 0)
        for zi in range(ZC):
            rows = [lines[f][zi * LINE : zi * LINE + count_a, :].astype(BF16) for f in range(fields)]
            wide = rows[0] if fields == 1 else jnp.concatenate(rows, axis=1)
            mixed = jnp.dot(kxs_ref[...], jnp.concatenate([wide, wide], axis=0), preferred_element_type=F32)
            for f in range(fields):
                img_ref[f, z0 + zi] = mixed[:count_a, f * 128 : (f + 1) * 128].astype(BF16)
            if on_rows is not None:
                carry = on_rows(z0 + zi, mixed[count_a : count_a + 8, :], carry)
        return carry

    zero = jnp.zeros((8, 128), F32)
    return lax.fori_loop(0, depth // ZC, chunk, (zero, zero))


def box_of(b, corner_ref, offs_ref):
    cx = corner_ref[0, b]
    cy = corner_ref[1, b]
    cz = corner_ref[2, b]
    x0 = pl.multiple_of(jnp.minimum((cx // 16) * 16, 128 - XW), 16)
    off = offs_ref[pl.ds(b, 1), :]
    row = (off & (BOXZ - 1)) * XW + (off >> 7) + (cx - x0)
    line = ((off >> 3) & (BOXY - 1)) + cy
    return x0, cz, row, line


def pick(fields, b, corner_ref, offs_ref, img_ref, iota_y, iota_r):
    x0, cz, row, line = box_of(b, corner_ref, offs_ref)
    boxes = [img_ref[f, pl.ds(cz, BOXZ), pl.ds(x0, XW), :].reshape(BOXZ * XW, 128) for f in range(fields)]
    box = boxes[0] if fields == 1 else jnp.concatenate(boxes, axis=0)
    onehot = jnp.where(iota_y == line, 1.0, 0.0).astype(BF16)
    lanes = jnp.dot(box, onehot, preferred_element_type=F32)
    wanted = iota_r == row
    n = BOXZ * XW
    return [
        jnp.sum(jnp.where(wanted, lanes[f * n : (f + 1) * n], 0.0), axis=0, keepdims=True)
        for f in range(fields)
    ]


def points_kernel(
    corner_ref,
    steps_ref,
    accept_ref,
    gath_ref,
    kxs_ref,
    own_ref,
    offs_ref,
    interp_ref,
    labels_ref,
    stats_ref,
    bend_scale_ref,
    spread_ref,
    line_u,
    line_v,
    img_ref,
    lat_ref,
    slope_ref,
    res_ref,
    acc_ref,
):
    blocks, _, cols = interp_ref.shape

    def on_rows(z, mixed, carry):
        own = own_ref[z]
        return (carry[0] + mixed[:, :128] * own, carry[1] + mixed[:, 128:] * own)

    quad_u, quad_v = depth_mix(2, gath_ref, kxs_ref, (line_u, line_v), img_ref, on_rows)
    iota_y = lax.broadcasted_iota(jnp.int32, (128, cols), 0)
    iota_r = lax.broadcasted_iota(jnp.int32, (BOXZ * XW, cols), 0)
    iota_8 = lax.broadcasted_iota(jnp.int32, (16, cols), 0)

    def gather_step(i, c):
        for u in range(UNROLL):
            b = i * UNROLL + u
            first, second = pick(2, b, corner_ref, offs_ref, img_ref, iota_y, iota_r)
            pair = jnp.where(iota_8 == 0, first, jnp.where(iota_8 == 1, second, 0.0)).astype(BF16)
            both = lax.dot_general(pair, interp_ref[b], NT, preferred_element_type=F32)
            lat_ref[pl.ds(b, 1), :] = both[0:1]
            slope_ref[pl.ds(b, 1), :] = both[1:2]
        return c

    lax.fori_loop(0, blocks // UNROLL, gather_step, 0)

    lat = lat_ref[...]
    slope = slope_ref[...]
    target = labels_ref[...].astype(F32)
    signed = 2.0 * target - 1.0
    stats_ref[...] = jnp.zeros_like(stats_ref)
    chosen = steps_ref[0]
    for k in range(1, NTRIAL):
        chosen = jnp.where(accept_ref[0] == k, steps_ref[k], chosen)
    for k in range(NTRIAL):
        q = lat + steps_ref[k] * slope
        s = signed * q
        loglik = jnp.minimum(s, 0.0) - jnp.log1p(jnp.exp(-jnp.abs(s)))
        stats_ref[k : k + 1, :] = jnp.sum(loglik, axis=0, keepdims=True)
        descent = (target - jax.nn.sigmoid(q)) * slope
        stats_ref[NTRIAL + k : NTRIAL + k + 1, :] = jnp.sum(descent, axis=0, keepdims=True)
    stats_ref[10:11, :] = quad_u[0:1] + quad_u[1:2]
    stats_ref[11:12, :] = quad_u[2:3] + quad_u[3:4]
    stats_ref[12:13, :] = quad_v[2:3] + quad_v[3:4]
    prob = jax.nn.sigmoid(lat + chosen * slope)
    bend_scale_ref[...] = prob * (1.0 - prob)
    res_ref[...] = (target - prob).astype(BF16).astype(F32)

    def clear(i, c):
        acc_ref[pl.ds(pl.multiple_of(i * LINE, 8), LINE), :] = jnp.zeros((LINE, 128), F32)
        return c

    lax.fori_loop(0, spread_ref.shape[1], clear, 0)

    def scatter_step(i, c):
        for u in range(UNROLL):
            b = i * UNROLL + u
            x0, cz, row, line = box_of(b, corner_ref, offs_ref)
            res = jnp.broadcast_to(res_ref[pl.ds(b, 1), :], (16, 128)).astype(BF16)
            term = jnp.dot(res, interp_ref[b], preferred_element_type=F32)[0:1]
            high = term.astype(BF16).astype(F32)
            low = term - high
            at_y = iota_y == line
            placed = jnp.concatenate([jnp.where(at_y, high, 0.0), jnp.where(at_y, low, 0.0)], axis=0).astype(BF16)
            onehot = jnp.where(iota_r == row, 1.0, 0.0).astype(BF16)
            both = lax.dot_general(onehot, placed, NT, preferred_element_type=F32)
            box = both[:, :128] + both[:, 128:]
            for d in range(BOXZ):
                at = pl.ds(pl.multiple_of((cz + d) * LINE + x0, 8), XW)
                acc_ref[at, :] = acc_ref[at, :] + box[d * XW : (d + 1) * XW]
        return c

    lax.fori_loop(0, blocks // UNROLL, scatter_step, 0)

    def emit(i, c):
        for u in range(4):
            x = i * 4 + u
            spread_ref[x] = acc_ref[pl.ds(x, spread_ref.shape[1], stride=LINE), :].astype(BF16)
        return c

    lax.fori_loop(0, spread_ref.shape[0] // 4, emit, 0)


UNROLL = 4


def bend_kernel(corner_ref, gath_ref, kxs_ref, offs_ref, interp_ref, scale_ref, curv_ref, line_u, img_ref):
    blocks, _, cols = interp_ref.shape
    depth_mix(1, gath_ref, kxs_ref, (line_u,), img_ref, None)
    iota_y = lax.broadcasted_iota(jnp.int32, (128, cols), 0)
    iota_r = lax.broadcasted_iota(jnp.int32, (BOXZ * XW, cols), 0)

    def step(i, c):
        for u in range(UNROLL):
            b = i * UNROLL + u
            (value,) = pick(1, b, corner_ref, offs_ref, img_ref, iota_y, iota_r)
            rows = jnp.broadcast_to(value, (16, cols)).astype(BF16)
            bend = lax.dot_general(rows, interp_ref[b], NT, preferred_element_type=F32)
            curv_ref[pl.ds(b, 1), :] = scale_ref[pl.ds(b, 1), :] * bend[0:1]
        return c

    lax.fori_loop(0, blocks // UNROLL, step, 0)


VM = pl.BlockSpec(memory_space=pltpu.VMEM)
SM = pl.BlockSpec(memory_space=pltpu.SMEM)


def split(values, count):
    terms = []
    for _ in range(count):
        high = lax.reduce_precision(values, 8, 7)
        terms.append(high.astype(BF16))
        values = values - high
    return terms


def split_pair(table):
    return jnp.concatenate(split(table, 2), axis=1)


def plane_of(fields, kern_y, kern_z):
    inner = jnp.einsum("fxbc,zc->fxbz", fields, kern_z, precision=HIGHEST)
    return jnp.einsum("fxbz,yb->xfzy", inner, kern_y, precision=HIGHEST).astype(BF16)


def body(
    grid_weights,
    direction,
    kern_x,
    kern_y,
    kern_z,
    interp,
    block_corner,
    block_offsets,
    labels,
    trial_steps,
    accept,
):
    slab, size_y, size_z = grid_weights.shape
    devices = lax.axis_size(PTS)
    size_x = slab * devices
    blocks, per_block, cols = interp.shape
    points = blocks * per_block * devices
    me = lax.axis_index(PTS)

    plane = plane_of(jnp.stack([grid_weights, direction]), kern_y, kern_z)
    gathered = lax.all_gather(plane, PTS, axis=0, tiled=True)
    mine = lax.dynamic_slice_in_dim(kern_x, me * slab, slab, 0)
    tall = jnp.concatenate([kern_x, mine, mine, jnp.zeros((16 - 2 * slab, size_x), F32)], axis=0)
    kxs = split_pair(tall)
    own = jnp.concatenate([grid_weights, direction], axis=0).transpose(2, 0, 1)
    own = jnp.pad(own, ((0, 0), (0, 8 - 2 * slab), (0, 0)))
    stats, bend_scale, spread_all = pl.pallas_call(
        points_kernel,
        name="points",
        in_specs=[SM, SM, SM, VM, VM, VM, VM, VM, VM],
        out_specs=[VM, VM, VM],
        out_shape=[
            jax.ShapeDtypeStruct((16, 128), F32),
            jax.ShapeDtypeStruct((blocks, per_block), F32),
            jax.ShapeDtypeStruct((size_x, size_z, size_y), BF16),
        ],
        scratch_shapes=[
            pltpu.VMEM(((ZC + 1) * LINE, 128), F32),
            pltpu.VMEM(((ZC + 1) * LINE, 128), F32),
            pltpu.VMEM((2, size_z, size_x, size_y), BF16),
            pltpu.VMEM((blocks, per_block), F32),
            pltpu.VMEM((blocks, per_block), F32),
            pltpu.VMEM((blocks, per_block), F32),
            pltpu.VMEM(((size_z + 1) * LINE, 128), F32),
        ],
        compiler_params=pltpu.CompilerParams(vmem_limit_bytes=VMEM_CAP),
    )(block_corner, trial_steps, accept, gathered, kxs, own, block_offsets, interp, labels)

    chosen = jnp.sum(jnp.where(jnp.arange(NTRIAL) == accept[0], trial_steps, 0.0))
    new_weights = grid_weights + chosen * direction
    pair = lax.axis_size(PTS[1])
    tiles = spread_all.reshape(devices // pair, pair, slab, size_z, size_y)
    tiles = lax.psum_scatter(jnp.moveaxis(tiles, 1, 0), PTS[1], scatter_dimension=0, tiled=True)[0]
    spread = lax.psum_scatter(tiles, PTS[0], scatter_dimension=0, tiled=True)[0]
    grid_gradient = spread.astype(F32).transpose(0, 2, 1) - new_weights

    bend_plane = plane_of(grid_gradient[None], kern_y, kern_z)
    tail = jnp.pad(jnp.stack(split(jnp.sum(stats, axis=1), 3), axis=1), ((0, 0), (0, size_y - 3)))
    tail = jnp.stack([tail] + [jnp.zeros_like(tail)] * (slab - 1))[:, None]
    bend_gathered = lax.all_gather(jnp.concatenate([bend_plane, tail], axis=2), PTS, axis=0, tiled=True)
    tails = bend_gathered.reshape(devices, slab, size_z + 16, size_y)[:, 0, size_z:, :3]
    sums = jnp.sum(tails.astype(F32), axis=(0, 2))
    loglik = sums[:NTRIAL]
    descent = sums[NTRIAL : 2 * NTRIAL]
    quad_gu, quad_du, quad_dv = sums[10], sums[11], sums[12]
    prior = 0.5 * (quad_gu + 2.0 * trial_steps * quad_du + trial_steps * trial_steps * quad_dv)
    trial_objective = (loglik - prior) / points
    trial_slope = (descent - quad_du - trial_steps * quad_dv) / points

    curvature = pl.pallas_call(
        bend_kernel,
        name="bend",
        in_specs=[SM, VM, VM, VM, VM, VM],
        out_specs=VM,
        out_shape=jax.ShapeDtypeStruct((blocks, per_block), F32),
        scratch_shapes=[
            pltpu.VMEM(((ZC + 1) * LINE, 128), F32),
            pltpu.VMEM((1, size_z, size_x, size_y), BF16),
        ],
        compiler_params=pltpu.CompilerParams(vmem_limit_bytes=VMEM_CAP),
    )(block_corner, bend_gathered, split_pair(kern_x), block_offsets, interp, bend_scale)
    return (new_weights, grid_gradient, curvature, trial_objective, trial_slope)


def solution(mesh):
    cores = 2
    chips = mesh.shape["pts"] // cores
    finer = Mesh(mesh.devices.reshape(mesh.shape["parts"], chips, cores), PARTS_PTS)
    placed = (
        P(PARTS_PTS, None, None),
        P(PARTS_PTS, None, None),
        P(),
        P(),
        P(),
        P(PARTS_PTS, None, None),
        P(None, PARTS_PTS),
        P(PARTS_PTS, None),
        P(PARTS_PTS, None),
        P(),
        P(),
    )
    return jax.shard_map(
        body,
        mesh=finer,
        in_specs=placed,
        out_specs=(
            P(PARTS_PTS, None, None),
            P(PARTS_PTS, None, None),
            P(PARTS_PTS, None),
            P("parts"),
            P("parts"),
        ),
        check_vma=False,
    )
```

time: 1220 us -> 595 us (0.49)
  local copies, waits for them, and re-layouts: 390 us -> 12.3 us
  other arithmetic: 338 us -> 9.57 us
  Pallas kernels: 0 us -> 120 us
  waiting for transfers between devices: 351 us -> 434 us
  blocking collectives: 77.9 us -> 0 us
  matrix products: 39.1 us -> 3.13 us
    gather x2 -> x0, local copies, waits for them, and re-layouts: 327 us -> none  [pick_cells(): taken = jnp.take(grid_rows, row_ids, axis=1)]
    scatter-add x1 -> x0, other arithmetic: 199 us -> none  [slab_add(): jnp.zeros((row_count * size_y, size_z), jnp.float32).at[target_row]]
    pallas_call x0 -> x2, Pallas kernels: none -> 120 us  [the longest x1 79.1 us: body(): pl.pallas_call(points_kernel, name='points', in_specs=[SM, SM, SM, VM, VM...]
    reduce_sum x4 -> x2, other arithmetic: 115 us -> 1.26 us  [the longest x1 1.15 us: body(): sums = jnp.sum(tails.astype(F32), axis=(0, 2))]
    all_gather x2, waiting for transfers between devices: 204 us -> 299 us  [the longest x1 153 us: body(): lax.all_gather(jnp.concatenate([bend_plane, tail], axis=2), PTS, axis=0,...]
    psum x2 -> x0, blocking collectives: 77.9 us -> none  [by_axis(): array = lax.psum(array, axis)]
    dot_general x9 -> x4, matrix products: 39.1 us -> 3.13 us  [the longest x2 1.63 us: plane_of(): inner = jnp.einsum('fxbc,zc->fxbz', fields, kern_z, precision=HIGHEST)]
    convert_element_type x3 -> x1, local copies, waits for them, and re-layouts: 17.4 us -> 0.66 us  [plane_of(): jnp.einsum('fxbz,yb->xfzy', inner, kern_y, precision=HIGHEST).astype(BF16)]
  transfers between devices with their start and end apart: 4 -> 4, of which waited for: 4 -> 4; matrix products, arithmetic and copies ran while one was open for 2% -> 1% of each run, Pallas kernels for 0% -> 0%
where the time goes in v1:
time: 595 us
  waiting for transfers between devices  434 us (73%)
  Pallas kernels  120 us (20%)
  between operations  15.2 us (3%)
  local copies, waits for them, and re-layouts  12.3 us (2%)
  other arithmetic  9.57 us (2%)
    all_gather x1, waiting for transfers between devices, body(): lax.all_gather(jnp.concatenate([bend_plane, tail], axis=2), PTS, axis=0,...  153 us
    all_gather x1, waiting for transfers between devices, body(): gathered = lax.all_gather(plane, PTS, axis=0, tiled=True)  146 us
    reduce_scatter x1, waiting for transfers between devices, body(): spread = lax.psum_scatter(tiles, PTS[0], scatter_dimension=0, tiled=True)[0]  114 us
    pallas_call x1, Pallas kernels, body(): pl.pallas_call(points_kernel, name='points', in_specs=[SM, SM, SM, VM, VM...  79.1 us
    pallas_call x1, Pallas kernels, body(): pl.pallas_call(bend_kernel, name='bend', in_specs=[SM, VM, VM, VM, VM, VM...  41.1 us
    reduce_scatter x1, waiting for transfers between devices, body(): lax.psum_scatter(jnp.moveaxis(tiles, 1, 0), PTS[1], scatter_dimension=0,...  20.9 us
  transfers between devices with their start and end apart: 4, of which 4 were waited for; matrix products, arithmetic and copies ran while one was open for 1% of the time, Pallas kernels for 0%

profile of v1, /device:TPU:37, one launch (start us, length us, event | category | flops | bytes accessed | tf_op | source)
XLA Modules:
  0.0 594.6 jit_solution(5904306006026069910)
XLA Ops:
  7.3 0.8 copy-done
  8.0 1.4 fusion.2
  9.4 1.2 fusion
  10.6 0.7 copy.22
  11.3 0.1 reduce-scatter.3.cloned.1.call-start
  11.4 1.0 copy.23
  12.4 1.0 copy.24
  14.1 0.1 maximum_bitcast_fusion
  14.3 0.9 pad.9.own_ref
  15.1 0.1 pad.25.clone
  15.2 0.7 constant_dynamic-slice_fusion
  15.9 0.9 reduce-precision_convert_fusion
  16.8 0.6 pad_maximum_fusion.kxs_ref
  17.5 145.6 %all-gather.3.cloned.1.call-done.gath_ref = bf16[128,2,128,128]{3,2,1,0:T(8,128)(2,1)} async-done(((bf16[2,2,128,128]{3,2,1,0:T(8,128)(2,1)}), bf16[128,2,128,128]{3,2,1,0:T(8,128)(2,1)}) %all-gather.3.cloned.1.call-update) | async-done | bytes 8388624 | tf_op jit(solution)/shard_map/all_gather | solution.py:246
  163.0 79.1 %points.1 = (f32[16,128]{1,0:T(8,128)}, f32[128,128]{1,0:T(8,128)}, bf16[128,128,128]{2,1,0:T(8,128)(2,1)}) custom-call(s32[3,128]{1,0:T(4,128)} %corner_ref.3, f32[5]{0:T(128)} %steps_ref.1, s32[1]{0:T(128)} %copy.30.accept_ref, bf16[128,2,128,128]{3,2,1,0:T(8,128)(2,1)} %all-gather.3.cloned.1.call-done.gath_ref, bf16[144,256]{1,0:T(8,128)(2,1)} %pad_maximum_fusion.kxs_ref, ...), custom_call_target="tpu_custom_call" | custom-call | tf_op jit(solution)/shard_map/points/pallas_call | solution.py:252
  242.1 6.4 %copy.25 = bf16[32,2,2,128,128]{3,4,2,0,1:T(8,128)(2,1)} copy(bf16[32,2,2,128,128]{4,3,2,1,0:T(8,128)(2,1)} %bitcast.62) | data formatting | bytes 8388608 | tf_op jit(solution)/shard_map/reshape | solution.py:277
  248.5 0.1 reduce-scatter.5.cloned.1.call-start
  248.6 20.9 %reduce-scatter.3.cloned.1.call-done = bf16[1,32,2,128,128]{3,4,2,1,0:T(8,128)(2,1)} async-done(((bf16[2,32,2,128,128]{3,4,2,1,0:T(8,128)(2,1)}), bf16[1,32,2,128,128]{3,4,2,1,0:T(8,128)(2,1)}) %reduce-scatter.3.cloned.1.call-update) | async-done | bytes 2097168 | tf_op jit(solution)/shard_map/reduce_scatter | solution.py:278
  269.7 0.6 fusion.18
  270.3 0.1 reduce_sum.30
  270.4 0.1 copy.26
  270.5 114.2 %reduce-scatter.5.cloned.1.call-done = bf16[1,2,128,128]{2,3,1,0:T(8,128)(2,1)} async-done(((bf16[32,2,128,128]{2,3,1,0:T(8,128)(2,1)}), bf16[1,2,128,128]{2,3,1,0:T(8,128)(2,1)}) %reduce-scatter.5.cloned.1.call-update) | async-done | bytes 65552 | tf_op jit(solution)/shard_map/reduce_scatter | solution.py:279
  384.8 2.2 fusion.6
  386.9 0.3 fusion.14
  387.2 0.3 fusion.1
  387.5 0.6 maximum_bitcast_fusion.1
  388.2 0.6 pad_maximum_fusion.1.kxs_ref
  388.9 153.1 %all-gather.5.cloned.1.call-done.gath_ref = bf16[128,1,144,128]{3,2,1,0:T(8,128)(2,1)} async-done(((bf16[2,1,144,128]{3,2,1,0:T(8,128)(2,1)}), bf16[128,1,144,128]{3,2,1,0:T(8,128)(2,1)}) %all-gather.5.cloned.1.call-update) | async-done | bytes 4718608 | tf_op jit(solution)/shard_map/all_gather | solution.py:285
  542.0 1.1 convert_reduce_fusion
  543.1 0.7 fusion.20
  544.4 2.6 subtract_multiply_fusion
  547.0 41.1 %bend.1 = f32[128,128]{1,0:T(8,128)} custom-call(s32[3,128]{1,0:T(4,128)} %corner_ref.3, bf16[128,1,144,128]{3,2,1,0:T(8,128)(2,1)} %all-gather.5.cloned.1.call-done.gath_ref, bf16[128,256]{1,0:T(8,128)(2,1)} %pad_maximum_fusion.1.kxs_ref, s32[128,256]{1,0:T(8,128)} %offs_ref.3, bf16[128,128,256]{2,1,0:T(8,128)(2,1)} %interp_ref.3, ...), custom_call_target="tpu_custom_call" | custom-call | tf_op jit(solution)/shard_map/bend/pallas_call | solution.py:295
  (27 shorter events, 0.4 us)
Async XLA Ops:
  7.2 0.8 copy-start
  7.2 155.8 %all-gather.3.cloned.1.call-start = ((), (), s32[]{:S(2)}) async-start(), calls=%async_computation.2 | async-start | bytes 8519680 | tf_op jit(solution)/shard_map/all_gather | solution.py:246
  11.3 258.2 %reduce-scatter.3.cloned.1.call-start = ((), (), s32[]{:S(2)}) async-start(), calls=%async_computation.3 | async-start | bytes 6291456 | tf_op jit(solution)/shard_map/reduce_scatter | solution.py:278
  248.4 21.2 %copy-start.7 = (f32[5]{0:T(128)S(1)}, f32[5]{0:T(128)}, u32[]{:S(2)}) copy-start(f32[5]{0:T(128)} %steps_ref.1) | copy-start | bytes 64
  248.4 21.8 %copy-start.6 = (f32[16,128]{1,0:T(8,128)S(1)}, f32[16,128]{1,0:T(8,128)}, u32[]{:S(2)}) copy-start(f32[16,128]{1,0:T(8,128)} %get-tuple-element.9) | copy-start | bytes 24580
  248.4 136.3 %copy-start.1 = (f32[2,128,128]{2,1,0:T(8,128)S(1)}, f32[2,128,128]{2,1,0:T(8,128)}, u32[]{:S(2)}) copy-start(f32[2,128,128]{2,1,0:T(8,128)} %param.12) | copy-start | bytes 393220
  248.4 136.3 %copy-start.2 = (f32[2,128,128]{2,1,0:T(8,128)S(1)}, f32[2,128,128]{2,1,0:T(8,128)}, u32[]{:S(2)}) copy-start(f32[2,128,128]{2,1,0:T(8,128)} %param.11) | copy-start | bytes 393220
  248.5 138.7 %copy-start.5 = (f32[128,128]{1,0:T(8,128)S(1)}, f32[128,128]{1,0:T(8,128)}, u32[]{:S(2)}) copy-start(f32[128,128]{1,0:T(8,128)} %param.14) | copy-start | bytes 196612
  248.5 139.7 %copy-start.4 = (f32[128,128]{1,0:T(8,128)S(1)}, f32[128,128]{1,0:T(8,128)}, u32[]{:S(2)}) copy-start(f32[128,128]{1,0:T(8,128)} %param.13) | copy-start | bytes 196612
  248.5 136.2 %reduce-scatter.5.cloned.1.call-start = ((), (), s32[]{:S(2)}) async-start(), calls=%async_computation.4 | async-start | bytes 2162688 | tf_op jit(solution)/shard_map/reduce_scatter | solution.py:279
  269.6 272.4 %all-gather.5.cloned.1.call-start = ((), (), s32[]{:S(2)}) async-start(), calls=%async_computation.5 | async-start | bytes 4792320 | tf_op jit(solution)/shard_map/all_gather | solution.py:285
  386.9 201.2 %copy-start.3 = (f32[2,128,128]{2,1,0:T(8,128)}, f32[2,128,128]{2,1,0:T(8,128)S(1)}, u32[]{:S(2)}) copy-start(f32[2,128,128]{2,1,0:T(8,128)S(1)} %get-tuple-element.11) | copy-start | bytes 393220
Sparse Core Ops, SparseCore 0:
  11.5 151.5 all-gather.2
  248.7 20.7 reduce-scatter.2
  272.1 112.6 reduce-scatter.4
  388.3 153.6 all-gather.4

commit v2 on v1

--- a/solution.py
+++ b/solution.py
@@ -21,6 +21,7 @@
 ZC = 16
 XW = 32
 VMEM_CAP = 60 * 1024 * 1024
+MESH = pl.DeviceIdType.MESH
 NT = (((1,), (1,)), ((), ()))
 
 
@@ -204,6 +205,235 @@
 SM = pl.BlockSpec(memory_space=pltpu.SMEM)
 
 
+def neighbours(ring):
+    chip = lax.axis_index(PTS[0])
+    core = lax.axis_index(PTS[1])
+    right = {PTS[0]: lax.rem(chip + 1, ring)}
+    left = {PTS[0]: lax.rem(chip + ring - 1, ring)}
+    mate = {PTS[1]: 1 - core}
+    return chip, core, (right, left), mate
+
+
+def greet(ways, mate):
+    barrier = pltpu.get_barrier_semaphore()
+    for other in (*ways, mate):
+        pl.semaphore_signal(barrier, inc=1, device_id=other, device_id_type=MESH)
+    pl.semaphore_wait(barrier, 3)
+
+
+def gather_kernel(ring, x_ref, out_ref, buf, send_sem, recv_sem, mate_send, mate_recv, out_sem):
+    chip, core, ways, mate = neighbours(ring)
+    chunks = x_ref.shape[0]
+    half = ring // 2
+    own = chip * 2 + core
+
+    def source(way, s):
+        return lax.rem(chip + ring - 1 - s, ring) if way == 0 else lax.rem(chip + 1 + s, ring)
+
+    def pass_on(way, s, slot, k, src):
+        return pltpu.make_async_remote_copy(
+            src_ref=src,
+            dst_ref=buf.at[slot, k],
+            send_sem=send_sem.at[way, s, k],
+            recv_sem=recv_sem.at[way, s, k],
+            device_id=ways[way],
+            device_id_type=MESH,
+        )
+
+    def hand_over(index, slot, k, src):
+        return pltpu.make_async_remote_copy(
+            src_ref=src,
+            dst_ref=buf.at[slot, k],
+            send_sem=mate_send.at[index, k],
+            recv_sem=mate_recv.at[index, k],
+            device_id=mate,
+            device_id_type=MESH,
+        )
+
+    greet(ways, mate)
+    for k in range(chunks):
+        for way in range(2):
+            pass_on(way, 0, own, k, x_ref.at[k]).start()
+    for k in range(chunks):
+        hand_over(ring - 1, own, k, x_ref.at[k]).start()
+    buf[own] = x_ref[...]
+
+    def receive(way, s, k, forward):
+        slot = source(way, s) * 2 + core
+        here = buf.at[slot, k]
+        pass_on(way, s, slot, k, here).wait_recv()
+        if forward:
+            pass_on(way, s + 1, slot, k, here).start()
+        hand_over(way * half + s, slot, k, here).start()
+
+    def step(s, c):
+        for k in range(chunks):
+            receive(0, s, k, True)
+            receive(1, s, k, True)
+        return c
+
+    lax.fori_loop(0, half - 2, step, 0)
+    for k in range(chunks):
+        receive(0, half - 2, k, True)
+        receive(1, half - 2, k, False)
+    for k in range(chunks):
+        receive(0, half - 1, k, False)
+
+    def settle(way, s):
+        slot = source(way, s) * 2 + core
+        theirs = source(way, s) * 2 + 1 - core
+        for k in range(chunks):
+            pass_on(way, s, slot, k, buf.at[slot, k]).wait_send()
+            hand_over(way * half + s, slot, k, buf.at[slot, k]).wait_send()
+            hand_over(way * half + s, theirs, k, buf.at[theirs, k]).wait_recv()
+
+    def settle_both(s, c):
+        settle(0, s)
+        settle(1, s)
+        return c
+
+    lax.fori_loop(0, half - 1, settle_both, 0)
+    settle(0, half - 1)
+    theirs = chip * 2 + 1 - core
+    for k in range(chunks):
+        hand_over(ring - 1, own, k, buf.at[own, k]).wait_send()
+        hand_over(ring - 1, theirs, k, buf.at[theirs, k]).wait_recv()
+    copy = pltpu.make_async_copy(buf, out_ref, out_sem)
+    copy.start()
+    copy.wait()
+
+
+def ring_gather(block, call):
+    ring = lax.axis_size(PTS[0])
+    chunks = block.shape[0]
+    return pl.pallas_call(
+        functools.partial(gather_kernel, ring),
+        name="ring_gather",
+        in_specs=[VM],
+        out_specs=pl.BlockSpec(memory_space=pl.ANY),
+        out_shape=jax.ShapeDtypeStruct((2 * ring, *block.shape), block.dtype),
+        scratch_shapes=[
+            pltpu.VMEM((2 * ring, *block.shape), block.dtype),
+            pltpu.SemaphoreType.DMA((2, ring // 2, chunks)),
+            pltpu.SemaphoreType.DMA((2, ring // 2, chunks)),
+            pltpu.SemaphoreType.DMA((ring, chunks)),
+            pltpu.SemaphoreType.DMA((ring, chunks)),
+            pltpu.SemaphoreType.DMA,
+        ],
+        compiler_params=pltpu.CompilerParams(
+            collective_id=call, has_side_effects=True, vmem_limit_bytes=VMEM_CAP
+        ),
+    )(block)
+
+
+def reduce_kernel(ring, x_ref, out_ref, mates, work, held, send_sem, recv_sem, mate_send, mate_recv):
+    chip, core, ways, mate = neighbours(ring)
+    chunks = x_ref.shape[2]
+    half = ring // 2
+
+    def target(way, s):
+        return lax.rem(chip + half - s, ring) if way == 0 else lax.rem(chip + half + 1 + s, ring)
+
+    def hand_over(index, t):
+        return pltpu.make_async_remote_copy(
+            src_ref=x_ref.at[t, 1 - core],
+            dst_ref=mates.at[t],
+            send_sem=mate_send.at[index],
+            recv_sem=mate_recv.at[index],
+            device_id=mate,
+            device_id_type=MESH,
+        )
+
+    def pass_on(way, s, k):
+        return pltpu.make_async_remote_copy(
+            src_ref=work.at[way, s, k],
+            dst_ref=held.at[way, s, k],
+            send_sem=send_sem.at[way, s, k],
+            recv_sem=recv_sem.at[way, s, k],
+            device_id=ways[way],
+            device_id_type=MESH,
+        )
+
+    greet(ways, mate)
+
+    def give(s, c):
+        hand_over(s, target(0, s)).start()
+        hand_over(half + s, target(1, s)).start()
+        return c
+
+    lax.fori_loop(0, half - 1, give, 0)
+    hand_over(half - 1, target(0, half - 1)).start()
+    hand_over(ring - 1, chip).start()
+
+    def local(t, k):
+        return x_ref[t, core, k].astype(F32) + mates[t, k].astype(F32)
+
+    def send(way, s, first):
+        t = target(way, s)
+        hand_over(way * half + s, t).wait_recv()
+        for k in range(chunks):
+            total = local(t, k)
+            if not first:
+                pass_on(way, s - 1, k).wait_recv()
+                total = total + held[way, s - 1, k].astype(F32)
+            work[way, s, k] = total.astype(BF16)
+            pass_on(way, s, k).start()
+
+    send(0, 0, True)
+    send(1, 0, True)
+
+    def step(s, c):
+        send(0, s, False)
+        send(1, s, False)
+        return c
+
+    lax.fori_loop(1, half - 1, step, 0)
+    send(0, half - 1, False)
+    hand_over(ring - 1, chip).wait_recv()
+    for k in range(chunks):
+        pass_on(1, half - 2, k).wait_recv()
+        pass_on(0, half - 1, k).wait_recv()
+        out_ref[k] = local(chip, k) + held[0, half - 1, k].astype(F32) + held[1, half - 2, k].astype(F32)
+
+    def settle(way, s):
+        hand_over(way * half + s, target(way, s)).wait_send()
+        for k in range(chunks):
+            pass_on(way, s, k).wait_send()
+
+    def settle_both(s, c):
+        settle(0, s)
+        settle(1, s)
+        return c
+
+    lax.fori_loop(0, half - 1, settle_both, 0)
+    settle(0, half - 1)
+    hand_over(ring - 1, chip).wait_send()
+
+
+def ring_reduce(blocks, call):
+    ring, _, *inside = blocks.shape
+    chunks = inside[0]
+    return pl.pallas_call(
+        functools.partial(reduce_kernel, ring),
+        name="ring_reduce",
+        in_specs=[VM],
+        out_specs=VM,
+        out_shape=jax.ShapeDtypeStruct(tuple(inside), F32),
+        scratch_shapes=[
+            pltpu.VMEM((ring, *inside), BF16),
+            pltpu.VMEM((2, ring // 2, *inside), BF16),
+            pltpu.VMEM((2, ring // 2, *inside), BF16),
+            pltpu.SemaphoreType.DMA((2, ring // 2, chunks)),
+            pltpu.SemaphoreType.DMA((2, ring // 2, chunks)),
+            pltpu.SemaphoreType.DMA((ring,)),
+            pltpu.SemaphoreType.DMA((ring,)),
+        ],
+        compiler_params=pltpu.CompilerParams(
+            collective_id=call, has_side_effects=True, vmem_limit_bytes=VMEM_CAP
+        ),
+    )(blocks)
+
+
 def split(values, count):
     terms = []
     for _ in range(count):
@@ -243,7 +473,8 @@
     me = lax.axis_index(PTS)
 
     plane = plane_of(jnp.stack([grid_weights, direction]), kern_y, kern_z)
-    gathered = lax.all_gather(plane, PTS, axis=0, tiled=True)
+    gathered = ring_gather(plane.reshape(2 * slab, size_z, size_y), 0)
+    gathered = gathered.reshape(size_x, 2, size_z, size_y)
     mine = lax.dynamic_slice_in_dim(kern_x, me * slab, slab, 0)
     tall = jnp.concatenate([kern_x, mine, mine, jnp.zeros((16 - 2 * slab, size_x), F32)], axis=0)
     kxs = split_pair(tall)
@@ -273,16 +504,15 @@
 
     chosen = jnp.sum(jnp.where(jnp.arange(NTRIAL) == accept[0], trial_steps, 0.0))
     new_weights = grid_weights + chosen * direction
-    pair = lax.axis_size(PTS[1])
-    tiles = spread_all.reshape(devices // pair, pair, slab, size_z, size_y)
-    tiles = lax.psum_scatter(jnp.moveaxis(tiles, 1, 0), PTS[1], scatter_dimension=0, tiled=True)[0]
-    spread = lax.psum_scatter(tiles, PTS[0], scatter_dimension=0, tiled=True)[0]
-    grid_gradient = spread.astype(F32).transpose(0, 2, 1) - new_weights
+    cores = lax.axis_size(PTS[1])
+    spread = ring_reduce(spread_all.reshape(devices // cores, cores, slab, size_z, size_y), 1)
+    grid_gradient = spread.transpose(0, 2, 1) - new_weights
 
     bend_plane = plane_of(grid_gradient[None], kern_y, kern_z)
     tail = jnp.pad(jnp.stack(split(jnp.sum(stats, axis=1), 3), axis=1), ((0, 0), (0, size_y - 3)))
     tail = jnp.stack([tail] + [jnp.zeros_like(tail)] * (slab - 1))[:, None]
-    bend_gathered = lax.all_gather(jnp.concatenate([bend_plane, tail], axis=2), PTS, axis=0, tiled=True)
+    bend_block = jnp.concatenate([bend_plane, tail], axis=2).reshape(-1, (size_z + 16) * slab // 3, size_y)
+    bend_gathered = ring_gather(bend_block, 2).reshape(size_x, 1, size_z + 16, size_y)
     tails = bend_gathered.reshape(devices, slab, size_z + 16, size_y)[:, 0, size_z:, :3]
     sums = jnp.sum(tails.astype(F32), axis=(0, 2))
     loglik = sums[:NTRIAL]

time: 595 us -> 348 us (0.58)
  waiting for transfers between devices: 434 us -> 0 us
  Pallas kernels: 120 us -> 327 us
  between operations: 15.2 us -> 2.12 us
  local copies, waits for them, and re-layouts: 12.3 us -> 4.98 us
    all_gather x2 -> x0, waiting for transfers between devices: 299 us -> none  [the longest x1 153 us: body(): lax.all_gather(jnp.concatenate([bend_plane, tail], axis=2), PTS, axis=0,...]
    pallas_call x0 -> x3, Pallas kernels: none -> 207 us  [the longest x2 159 us: ring_gather(): pl.pallas_call(functools.partial(gather_kernel, ring), name='ring_gather'...]
    reduce_scatter x2 -> x0, waiting for transfers between devices: 135 us -> none  [the longest x1 114 us: body(): spread = lax.psum_scatter(tiles, PTS[0], scatter_dimension=0, tiled=True)[0]]
    reshape x1 -> x0, local copies, waits for them, and re-layouts: 6.36 us -> none  [body(): tiles = spread_all.reshape(devices // pair, pair, slab, size_z, size_y)]
  transfers between devices with their start and end apart: 4 -> 0, of which waited for: 4 -> 0; matrix products, arithmetic and copies ran while one was open for 1% -> 0% of each run, Pallas kernels for 0% -> 0%
where the time goes in v2:
time: 348 us; the launch traced here: 347 us
  Pallas kernels  327 us (94%)
  other arithmetic  9.71 us (3%)
  local copies, waits for them, and re-layouts  4.98 us (1%)
    pallas_call x2, Pallas kernels, ring_gather(): pl.pallas_call(functools.partial(gather_kernel, ring), name='ring_gather'...  159 us
    pallas_call x1, Pallas kernels, body(): pl.pallas_call(points_kernel, name='points', in_specs=[SM, SM, SM, VM, VM...  79.1 us
    pallas_call x1, Pallas kernels, ring_reduce(): pl.pallas_call(functools.partial(reduce_kernel, ring), name='ring_reduce'...  47.8 us
    pallas_call x1, Pallas kernels, body(): pl.pallas_call(bend_kernel, name='bend', in_specs=[SM, VM, VM, VM, VM, VM...  41.1 us

profile of v2, /device:TPU:37, one launch (start us, length us, event | category | flops | bytes accessed | tf_op | source)
XLA Modules:
  0.0 347.4 jit_solution(389546895710460788)
XLA Ops:
  0.6 0.0 copy-start
  0.7 0.7 constant_dynamic-slice_fusion
  1.4 0.1 pad.25.clone
  1.5 0.9 reduce-precision_convert_fusion
  2.4 0.6 pad_maximum_fusion.kxs_ref
  3.7 1.4 fusion.2
  5.1 1.3 fusion
  6.4 0.7 copy.27
  7.0 88.9 %ring_gather.2 = bf16[64,4,128,128]{3,2,1,0:T(8,128)(2,1)} custom-call(bf16[4,128,128]{2,1,0:T(8,128)(2,1)} %bitcast.61), custom_call_target="tpu_custom_call" | custom-call | tf_op jit(solution)/shard_map/ring_gather/pallas_call | solution.py:309
  95.9 0.1 copy.28
  96.1 0.1 copy.29
  96.2 0.1 maximum_bitcast_fusion
  96.3 0.9 pad.9.own_ref
  97.2 79.1 %points.1 = (f32[16,128]{1,0:T(8,128)}, f32[128,128]{1,0:T(8,128)}, bf16[128,128,128]{2,1,0:T(8,128)(2,1)}) custom-call(s32[3,128]{1,0:T(4,128)} %corner_ref.3, f32[5]{0:T(128)} %steps_ref.1, s32[1]{0:T(128)} %copy.35.accept_ref, bf16[128,2,128,128]{3,2,1,0:T(8,128)(2,1)} %bitcast.55, bf16[144,256]{1,0:T(8,128)(2,1)} %pad_maximum_fusion.kxs_ref, ...), custom_call_target="tpu_custom_call" | custom-call | tf_op jit(solution)/shard_map/points/pallas_call | solution.py:483
  176.2 0.8 reduce_sum.30
  177.1 0.1 copy.30
  177.2 47.8 %ring_reduce.1 = f32[2,128,128]{2,1,0:T(8,128)} custom-call(bf16[32,2,2,128,128]{4,3,2,1,0:T(8,128)(2,1)} %bitcast.58), custom_call_target="tpu_custom_call" | custom-call | tf_op jit(solution)/shard_map/ring_reduce/pallas_call | solution.py:416
  225.1 0.6 fusion.17
  225.7 0.1 copy.25
  225.8 0.1 copy.26
  225.9 1.6 bitcast_subtract_fusion
  227.4 0.3 fusion.13
  227.7 0.3 fusion.1
  228.0 0.6 pad_maximum_fusion.1
  228.7 70.5 %ring_gather.3 = bf16[64,3,96,128]{3,2,1,0:T(8,128)(2,1)} custom-call(bf16[3,96,128]{2,1,0:T(8,128)(2,1)} %bitcast.62), custom_call_target="tpu_custom_call" | custom-call | tf_op jit(solution)/shard_map/ring_gather/pallas_call | solution.py:309
  299.2 1.2 convert_reduce_fusion
  300.4 0.6 fusion.19
  301.6 2.5 subtract_multiply_fusion
  304.2 0.6 pad_maximum_fusion.2.kxs_ref
  304.8 41.1 %bend.1 = f32[128,128]{1,0:T(8,128)} custom-call(s32[3,128]{1,0:T(4,128)} %corner_ref.3, bf16[128,1,144,128]{3,2,1,0:T(8,128)(2,1)} %bitcast.57, bf16[128,256]{1,0:T(8,128)(2,1)} %pad_maximum_fusion.2.kxs_ref, s32[128,256]{1,0:T(8,128)} %offs_ref.3, bf16[128,128,256]{2,1,0:T(8,128)(2,1)} %interp_ref.3, f32[128,128]{1,0:T(8,128)} %get-tuple-element.10.scale_ref), custom_call_target="tpu_custom_call" | custom-call | tf_op jit(solution)/shard_map/bend/pallas_call | solution.py:525
  345.9 0.8 copy.32
  346.7 0.8 copy.31
  (17 shorter events, 0.1 us)
Async XLA Ops:
  0.6 3.1 copy-start
  5.1 90.9 %copy-start.2 = (f32[2,128,128]{2,1,0:T(8,128)S(1)}, f32[2,128,128]{2,1,0:T(8,128)}, u32[]{:S(2)}) copy-start(f32[2,128,128]{2,1,0:T(8,128)} %param.11) | copy-start | bytes 393220
  5.1 91.0 %copy-start.1 = (f32[2,128,128]{2,1,0:T(8,128)S(1)}, f32[2,128,128]{2,1,0:T(8,128)}, u32[]{:S(2)}) copy-start(f32[2,128,128]{2,1,0:T(8,128)} %param.12) | copy-start | bytes 393220
  97.2 127.9 %copy-start.5 = (f32[5]{0:T(128)S(1)}, f32[5]{0:T(128)}, u32[]{:S(2)}) copy-start(f32[5]{0:T(128)} %steps_ref.1) | copy-start | bytes 64
  176.2 51.5 %copy-start.4 = (f32[128,128]{1,0:T(8,128)S(1)}, f32[128,128]{1,0:T(8,128)}, u32[]{:S(2)}) copy-start(f32[128,128]{1,0:T(8,128)} %param.14) | copy-start | bytes 196612
  177.2 126.9 %copy-start.3 = (f32[128,128]{1,0:T(8,128)S(1)}, f32[128,128]{1,0:T(8,128)}, u32[]{:S(2)}) copy-start(f32[128,128]{1,0:T(8,128)} %param.13) | copy-start | bytes 196612
